TPU v7x, 32 devices: a whole 2x2x4 slice. The times are simulated.
32 devices in a mesh: rep: 4 (over y, core), shard: 8 (over z, x).
Axes of the slice: x: 2, y: 2, z: 4, core: 2. Of those that a mesh axis runs over, the one named last changes fastest.
Arguments:
- hidden: bfloat16 [14336, 3584], P(('rep', 'shard')), may hold values from -144 to 144
- cotangent: bfloat16 [14336, 1024], P(('rep', 'shard')), may hold values from -6 to 6
- seq_ids: int32 [32, 448], P(('rep', 'shard')), may hold values from 0 to 3, as said below
- response_mask: int32 [32, 448], P(('rep', 'shard')), may hold values from 0 to 1, as said below
- group_ids: int32 [32, 4], P(('rep', 'shard')), may hold values from 0 to 15
- rewards: float32 [32, 4], P(('rep', 'shard')), may hold values from -6 to 6
- new_logp: float32 [32, 448], P(('rep', 'shard')), may hold values from -1.5 to -0.1
- old_logp: float32 [32, 448], P(('rep', 'shard')), may hold values from -1.5 to -0.1
- ref_logp: float32 [32, 448], P(('rep', 'shard')), may hold values from -1.5 to -0.1
- master: float32 [3, 3584, 1024], P(None, 'shard'), may hold values from -6 to 6
Outputs:
- new_master: float32 [3584, 1024], P('shard')
- rollout: bfloat16 [3, 3584, 2048], P(None, None, 'shard')
Inputs may be any that keep to these rules, and one draw needn't show every extreme that they name: `seq_ids`: each row numbers its device's 4 sequences in token order, never falling, each with one token or more. `response_mask`: within a sequence, prompt tokens come before response tokens; a sequence may have no response tokens.
All inputs are finite; a program needn't handle non-finite values.
Results may differ from a plain program's by a relative error of at most 0.0095.
Values may be sent and summed in bfloat16 or wider, within the bound.
A program may use at most 128 MiB of HBM per device.

v0:
```python
import jax
import jax.numpy as jnp
from jax import lax
from jax.sharding import PartitionSpec as P

HEAD = 128
KV_HEADS = 4
TP = 8
SEQ_DEV = 4


def token_coef(seq_row, mask_row, adv_row, new_row, old_row, ref_row):
    onehot = (seq_row[:, None] == jnp.arange(SEQ_DEV, dtype=jnp.int32)[None, :]).astype(jnp.float32)
    maskf = mask_row.astype(jnp.float32)
    lengths = jnp.maximum(jnp.dot(maskf, onehot, precision=lax.Precision.HIGHEST), 1.0)
    tok_len = jnp.dot(onehot, lengths, precision=lax.Precision.HIGHEST)
    tok_adv = jnp.dot(onehot, adv_row, precision=lax.Precision.HIGHEST)
    surrogate = -tok_adv * jnp.exp(new_row - old_row) + 0.2 * (1.0 - jnp.exp(ref_row - new_row))
    return maskf / tok_len * surrogate


def group_advantage(group_flat, reward_flat, stats):
    groups = stats.shape[1]
    onehot = (group_flat[:, None] == jnp.arange(groups, dtype=jnp.int32)[None, :]).astype(
        jnp.float32
    )
    count = jnp.maximum(stats[0], 1.0)
    mean = stats[1] / count
    spread = jnp.sqrt(jnp.maximum(stats[2] / count - mean * mean, 0.0))
    tok_mean = jnp.dot(onehot, mean, precision=lax.Precision.HIGHEST)
    tok_std = jnp.dot(onehot, jnp.maximum(spread, 0.5), precision=lax.Precision.HIGHEST)
    return (reward_flat - tok_mean) / tok_std


def group_sums(group_flat, reward_flat, groups):
    onehot = (group_flat[:, None] == jnp.arange(groups, dtype=jnp.int32)[None, :]).astype(
        jnp.float32
    )
    values = jnp.stack([jnp.ones_like(reward_flat), reward_flat, reward_flat * reward_flat], axis=0)
    return jnp.dot(values, onehot, precision=lax.Precision.HIGHEST)


def rounded(term):
    return lax.optimization_barrier(term.astype(jnp.bfloat16)).astype(jnp.float32)


def rollout_blocks(weights):
    layer_count = weights.shape[0]
    row_count = weights.shape[1]
    paired = weights.reshape(layer_count, row_count, 2, KV_HEADS, HEAD).transpose(0, 1, 3, 2, 4)
    paired = paired.reshape(layer_count, row_count, KV_HEADS, 2 * HEAD)
    by_rank = jnp.repeat(paired, TP // KV_HEADS, axis=2)
    copies = jnp.tile(by_rank, (1, 1, lax.axis_size("shard") // TP, 1))
    return copies.reshape(layer_count, row_count, lax.axis_size("shard") * 2 * HEAD)


def per_device(
    hidden,
    cotangent,
    seq_ids,
    response_mask,
    group_ids,
    rewards,
    new_logp,
    old_logp,
    ref_logp,
    master,
):
    n_rep = lax.axis_size("rep")
    n_shard = lax.axis_size("shard")
    groups = n_rep * n_shard * SEQ_DEV // 8
    rest_cols = lax.all_to_all(
        rollout_blocks(master[1:].astype(jnp.bfloat16)),
        "shard",
        split_axis=2,
        concat_axis=1,
        tiled=True,
    )
    local_sums = group_sums(group_ids[0], rewards[0], groups)
    stats = lax.psum(local_sums, ("rep", "shard"))
    advantage = group_advantage(group_ids[0], rewards[0], stats)
    coef = token_coef(
        seq_ids[0], response_mask[0], advantage, new_logp[0], old_logp[0], ref_logp[0]
    )
    delta = (coef[:, None] * cotangent.astype(jnp.float32)).astype(jnp.bfloat16)
    feature_count = hidden.shape[1]
    partial_value = lax.psum_scatter(
        rounded(
            lax.dot_general(
                hidden, delta, (((0,), (0,)), ((), ())), preferred_element_type=jnp.float32
            )
        ).astype(jnp.bfloat16),
        "shard",
        scatter_dimension=0,
        tiled=True,
    )
    grad = lax.psum(partial_value, "rep").astype(jnp.float32)
    squares = lax.psum(jnp.sum(grad * grad), "shard")
    rms = jnp.sqrt(squares / (feature_count * grad.shape[1]) + 1e-06)
    new_master = master[0] - 0.5 * grad / rms
    first_cols = lax.all_to_all(
        rollout_blocks(new_master[None].astype(jnp.bfloat16)),
        "shard",
        split_axis=2,
        concat_axis=1,
        tiled=True,
    )
    rollout = jnp.concatenate([first_cols, rest_cols], axis=0)
    return (new_master, rollout)


def solution(mesh):
    in_specs = (
        P(("rep", "shard"), None),
        P(("rep", "shard"), None),
        P(("rep", "shard"), None),
        P(("rep", "shard"), None),
        P(("rep", "shard"), None),
        P(("rep", "shard"), None),
        P(("rep", "shard"), None),
        P(("rep", "shard"), None),
        P(("rep", "shard"), None),
        P(None, "shard", None),
    )
    out_specs = (P("shard", None), P(None, None, "shard"))
    return jax.shard_map(
        per_device, mesh=mesh, in_specs=in_specs, out_specs=out_specs, check_vma=False
    )
```

profile of v0, /device:TPU:0, one launch (start us, length us, event | category | flops | bytes accessed | tf_op | source)
XLA Modules:
  0.0 468.4 jit_solution(8274017862780211825)
XLA Ops:
  9.0 41.9 %psum.21 = f32[3,16]{1,0:T(4,128)S(1)} all-reduce(f32[3,16]{1,0:T(4,128)S(1)} %fusion.15), channel_id=1, replica_groups=mesh['rep'=4,'shard'=8] {'rep','shard'}, use_global_device_ids=true, to_apply=%region_0.0 | all-reduce | flops 48 | bytes 384 | tf_op jit(solution)/shard_map/psum | solution.py:80
  57.1 7.5 %fusion = bf16[3584,1024]{0,1:T(8,128)(2,1)} fusion(bf16[448,3584]{1,0:T(8,128)(2,1)S(1)} %copy-done, bf16[448,1024]{1,0:T(8,128)(2,1)} %param.11, f32[448]{0:T(512)S(1)} %add_multiply_fusion), kind=kOutput, calls=%fused_computation.1 | convolution fusion | flops 3293380608 | bytes 11470592 | tf_op jit(solution)/shard_map/dot_general | solution.py:89
  64.6 10.4 %copy.47 = bf16[3584,1024]{1,0:T(8,128)(2,1)} copy(bf16[3584,1024]{0,1:T(8,128)(2,1)} %fusion) | data formatting | bytes 14680064
  79.6 5.7 %copy.49 = bf16[2,448,2,4,128]{1,0,4,2,3:T(2,128)(2,1)S(1)} copy(bf16[2,448,2,4,128]{4,3,2,1,0:T(4,128)(2,1)} %reshape.41) | data formatting | bytes 3670016 | tf_op jit(solution)/shard_map/transpose | solution.py:50
  85.3 4.2 broadcast_in_dim.15
  89.5 5.3 %all-to-all-start.1 = ((bf16[2,448,2048]{1,0,2:T(2,128)(2,1)}), bf16[2,448,2048]{1,0,2:T(2,128)(2,1)}, u32[]{:S(2)}, u32[]{:S(2)}) async-start(bf16[2,448,2048]{1,0,2:T(2,128)(2,1)} %bitcast.83), calls=%async_computation.1 | async-start | bytes 8388608 | tf_op jit(solution)/shard_map/all_to_all | solution.py:72
  94.9 188.3 %reduce-scatter.4.cloned.1.call-done = bf16[448,1024]{1,0:T(8,128)(2,1)} async-done(((bf16[3584,1024]{1,0:T(8,128)(2,1)}), bf16[448,1024]{1,0:T(8,128)(2,1)}) %reduce-scatter.4.cloned.1.call-update) | async-done | bytes 917520
  285.4 36.1 %all-reduce.2.cloned.1.call-done = bf16[448,1024]{0,1:T(8,128)(2,1)} async-done(((bf16[448,1024]{0,1:T(8,128)(2,1)}), bf16[448,1024]{0,1:T(8,128)(2,1)}) %all-reduce.2.cloned.1.call-update) | async-done | bytes 917520 | tf_op jit(solution)/shard_map/psum | solution.py:97
  325.7 22.1 %psum.23 = f32[]{:T(128)} all-reduce(f32[]{:T(128)} %fusion.3), channel_id=1, replica_groups=mesh['rep'=4,'shard'=8] {'shard'}, use_global_device_ids=true, to_apply=%region_4.0 | all-reduce | flops 1 | bytes 8 | tf_op jit(solution)/shard_map/psum | solution.py:98
  348.6 3.0 fusion.36
  351.6 3.6 copy.33
  355.2 2.7 reshape.40
  358.6 2.5 broadcast_in_dim.6
  361.1 5.3 %broadcast_in_dim.14 = bf16[1,448,2048]{2,1,0:T(8,128)(2,1)} reshape(bf16[448,4,2,256]{3,2,1,0:T(2,128)(2,1)} %broadcast_in_dim.6) | data formatting | bytes 3670016 | tf_op jit(solution)/shard_map/broadcast_in_dim | solution.py:52
  366.4 10.7 %copy.35 = bf16[1,448,2048]{1,0,2:T(2,128)(2,1)} copy(bf16[1,448,2048]{2,1,0:T(8,128)(2,1)} %broadcast_in_dim.14) | data formatting | bytes 3670016 | tf_op jit(solution)/shard_map/broadcast_in_dim | solution.py:52
  377.6 15.4 %reduce = bf16[2048,448]{1,0:T(8,128)(2,1)} reduce(bf16[2048,1,448]{2,1,0:T(2,128)(2,1)} %bitcast.84, bf16[]{:T(256)} %broadcast.50), dimensions={1}, to_apply=%bitcast.77.reduce_sub_computation | reduce | bytes 3670018
  393.1 6.8 %reshape.57 = bf16[8,2,57344]{2,1,0:T(2,128)(2,1)} reshape(bf16[2048,448]{1,0:T(8,128)(2,1)} %reduce) | data formatting | bytes 3670016
  399.8 4.3 all-to-all-start
  404.2 11.1 %copy.46 = bf16[2,448,8,256]{3,1,2,0:T(8,128)(2,1)} copy(bf16[2,448,8,256]{1,0,3,2:T(2,128)(2,1)} %bitcast.27) | data formatting | bytes 7340032 | tf_op jit(solution)/shard_map/all_to_all | solution.py:72
  417.0 25.9 %all-to-all-done = bf16[8,2,57344]{2,1,0:T(2,128)(2,1)} async-done(((bf16[8,2,57344]{2,1,0:T(2,128)(2,1)}), bf16[8,2,57344]{2,1,0:T(2,128)(2,1)}, u32[]{:S(2)}, u32[]{:S(2)}) %all-to-all-start) | async-done | bytes 1835040 | tf_op jit(solution)/shard_map/all_to_all | solution.py:101
  442.9 7.2 %reshape.58 = bf16[2048,1,448]{2,1,0:T(2,128)(2,1)} reshape(bf16[8,2,57344]{2,1,0:T(2,128)(2,1)} %all-to-all-done) | data formatting | bytes 3670016
  450.1 2.8 copy.50
  452.9 3.0 copy.43
  458.4 2.9 pad_maximum_fusion
  (36 shorter events, 24.8 us)
Async XLA Ops:
  7.2 49.9 %copy-start = (bf16[448,3584]{1,0:T(8,128)(2,1)S(1)}, bf16[448,3584]{1,0:T(8,128)(2,1)}, u32[]{:S(2)}) copy-start(bf16[448,3584]{1,0:T(8,128)(2,1)} %param.10) | copy-start | bytes 9633796
  7.2 276.0 %reduce-scatter.4.cloned.1.call-start = ((), (), s32[]{:S(2)}) async-start(), calls=%async_computation.4 | async-start | bytes 8257536
  89.5 310.4 %all-to-all-start.1 = ((bf16[2,448,2048]{1,0,2:T(2,128)(2,1)}), bf16[2,448,2048]{1,0,2:T(2,128)(2,1)}, u32[]{:S(2)}, u32[]{:S(2)}) async-start(bf16[2,448,2048]{1,0,2:T(2,128)(2,1)} %bitcast.83), calls=%async_computation.1 | async-start | bytes 8388608 | tf_op jit(solution)/shard_map/all_to_all | solution.py:72
  94.8 226.7 %all-reduce.2.cloned.1.call-start = ((), (), s32[]{:S(2)}) async-start(), calls=%async_computation.3 | async-start | bytes 2097152 | tf_op jit(solution)/shard_map/psum | solution.py:97
  285.4 38.5 %slice-start = ((f32[3,448,1024]{2,1,0:T(8,128)}), f32[1,448,1024]{2,1,0:T(8,128)S(1)}, s32[]{:S(2)}) async-start(f32[3,448,1024]{2,1,0:T(8,128)} %param.19), calls=%async_computation.5 | async-start | bytes 3670016 | tf_op jit(solution)/shard_map/slice | solution.py:100
  323.9 24.7 %copy-start.3 = (bf16[448,1024]{0,1:T(8,128)(2,1)S(1)}, bf16[448,1024]{0,1:T(8,128)(2,1)}, u32[]{:S(2)}) copy-start(bf16[448,1024]{0,1:T(8,128)(2,1)} %all-reduce.2.cloned.1.call-done) | copy-start | bytes 2752516
  399.8 43.1 %all-to-all-start = ((bf16[8,2,57344]{2,1,0:T(2,128)(2,1)}), bf16[8,2,57344]{2,1,0:T(2,128)(2,1)}, u32[]{:S(2)}, u32[]{:S(2)}) async-start(bf16[8,2,57344]{2,1,0:T(2,128)(2,1)} %reshape.57), calls=%async_computation | async-start | bytes 3670016 | tf_op jit(solution)/shard_map/all_to_all | solution.py:101
  455.8 2.6 copy-start.2
  458.4 3.1 copy-start.1
Sparse Core Ops, SparseCore 0:
  75.2 207.9 reduce-scatter.3
  286.1 35.3 all-reduce.1
where the time goes:
time: 470 us; the launch traced here: 468 us
  waiting for transfers between devices  250 us (53%)
  local copies, waits for them, and re-layouts  90.3 us (19%)
  blocking collectives  64.1 us (14%)
  other arithmetic  26 us (6%)
  between operations  14.8 us (3%)
  matrix products  13.1 us (3%)
  starting transfers between devices  9.74 us (2%)
    unnamed x3, waiting for transfers between devices  188 us
    psum x1, blocking collectives, per_device(): stats = lax.psum(local_sums, ('rep', 'shard'))  41.9 us
    psum x1, waiting for transfers between devices, per_device(): grad = lax.psum(partial_value, 'rep').astype(jnp.float32)  36.1 us
    unnamed x16, local copies, waits for them, and re-layouts  34.2 us
    all_to_all x1, waiting for transfers between devices, per_device(): lax.all_to_all(rollout_blocks(new_master[None].astype(jnp.bfloat16)), 'sh...  25.9 us
    broadcast_in_dim x4, local copies, waits for them, and re-layouts, rollout_blocks(): by_rank = jnp.repeat(paired, TP // KV_HEADS, axis=2)  22.7 us
    psum x1, blocking collectives, per_device(): squares = lax.psum(jnp.sum(grad * grad), 'shard')  22.1 us
    unnamed x1, other arithmetic  15.4 us
  transfers between devices with their start and end apart: 4, of which 3 were waited for; matrix products, arithmetic and copies ran while one was open for 18% of the time, Pallas kernels for 0%

commit v1 on v0

--- a/solution.py
+++ b/solution.py
@@ -77,7 +77,8 @@
         tiled=True,
     )
     local_sums = group_sums(group_ids[0], rewards[0], groups)
-    stats = lax.psum(local_sums, ("rep", "shard"))
+    inner = lax.psum(local_sums, "shard")
+    stats = lax.psum(inner, "rep")
     advantage = group_advantage(group_ids[0], rewards[0], stats)
     coef = token_coef(
         seq_ids[0], response_mask[0], advantage, new_logp[0], old_logp[0], ref_logp[0]

time: 470 us -> 450 us (0.957)
  blocking collectives: 64.1 us -> 50.9 us
  waiting for transfers between devices: 250 us -> 244 us
    psum x1 -> x2, blocking collectives: 41.9 us -> 28.8 us  [the longest x1 23.1 us: per_device(): inner = lax.psum(local_sums, 'shard')]
    unnamed x3, waiting for transfers between devices: 188 us -> 182 us
  transfers between devices with their start and end apart: 4 -> 4, of which waited for: 3 -> 3; matrix products, arithmetic and copies ran while one was open for 18% -> 19% of each run, Pallas kernels for 0% -> 0%
where the time goes in v1:
time: 450 us; the launch traced here: 448 us
  waiting for transfers between devices  244 us (54%)
  local copies, waits for them, and re-layouts  90.2 us (20%)
  blocking collectives  50.9 us (11%)
  other arithmetic  26.1 us (6%)
  between operations  14.8 us (3%)
  matrix products  13.2 us (3%)
  starting transfers between devices  8.95 us (2%)
    unnamed x3, waiting for transfers between devices  182 us
    psum x1, waiting for transfers between devices, per_device(): grad = lax.psum(partial_value, 'rep').astype(jnp.float32)  36.1 us
    unnamed x16, local copies, waits for them, and re-layouts  34.2 us
    all_to_all x1, waiting for transfers between devices, per_device(): lax.all_to_all(rollout_blocks(new_master[None].astype(jnp.bfloat16)), 'sh...  25.9 us
    psum x1, blocking collectives, per_device(): inner = lax.psum(local_sums, 'shard')  23.1 us
    broadcast_in_dim x4, local copies, waits for them, and re-layouts, rollout_blocks(): by_rank = jnp.repeat(paired, TP // KV_HEADS, axis=2)  22.6 us
    psum x1, blocking collectives, per_device(): squares = lax.psum(jnp.sum(grad * grad), 'shard')  22.1 us
    unnamed x1, other arithmetic  15.4 us
  transfers between devices with their start and end apart: 4, of which 3 were waited for; matrix products, arithmetic and copies ran while one was open for 19% of the time, Pallas kernels for 0%

profile of v1, /device:TPU:0, one launch (start us, length us, event | category | flops | bytes accessed | tf_op | source)
XLA Modules:
  0.0 447.9 jit_solution(14015395834165962103)
XLA Ops:
  9.0 23.1 %psum.28 = f32[3,16]{1,0:T(4,128)S(1)} all-reduce(f32[3,16]{1,0:T(4,128)S(1)} %fusion.15), channel_id=1, replica_groups=mesh['rep'=4,'shard'=8] {'shard'}, use_global_device_ids=true, to_apply=%region_0.0 | all-reduce | flops 48 | bytes 384 | tf_op jit(solution)/shard_map/psum | solution.py:80
  32.1 5.6 %psum.29 = f32[3,16]{1,0:T(4,128)S(1)} all-reduce(f32[3,16]{1,0:T(4,128)S(1)} %psum.28), channel_id=1, replica_groups=mesh['rep'=4,'shard'=8] {'rep'}, use_global_device_ids=true, to_apply=%region_1.0 | all-reduce | flops 48 | bytes 384 | tf_op jit(solution)/shard_map/psum | solution.py:81
  43.9 7.5 %fusion = bf16[3584,1024]{0,1:T(8,128)(2,1)} fusion(bf16[448,3584]{1,0:T(8,128)(2,1)S(1)} %copy-done, bf16[448,1024]{1,0:T(8,128)(2,1)} %param.11, f32[448]{0:T(512)S(1)} %add_multiply_fusion), kind=kOutput, calls=%fused_computation.1 | convolution fusion | flops 3293380608 | bytes 11470592 | tf_op jit(solution)/shard_map/dot_general | solution.py:90
  51.5 10.4 %copy.47 = bf16[3584,1024]{1,0:T(8,128)(2,1)} copy(bf16[3584,1024]{0,1:T(8,128)(2,1)} %fusion) | data formatting | bytes 14680064
  66.5 5.7 %copy.49 = bf16[2,448,2,4,128]{1,0,4,2,3:T(2,128)(2,1)S(1)} copy(bf16[2,448,2,4,128]{4,3,2,1,0:T(4,128)(2,1)} %reshape.41) | data formatting | bytes 3670016 | tf_op jit(solution)/shard_map/transpose | solution.py:50
  72.2 4.2 broadcast_in_dim.15
  76.4 4.5 %all-to-all-start.1 = ((bf16[2,448,2048]{1,0,2:T(2,128)(2,1)}), bf16[2,448,2048]{1,0,2:T(2,128)(2,1)}, u32[]{:S(2)}, u32[]{:S(2)}) async-start(bf16[2,448,2048]{1,0,2:T(2,128)(2,1)} %bitcast.83), calls=%async_computation.1 | async-start | bytes 8388608 | tf_op jit(solution)/shard_map/all_to_all | solution.py:72
  81.0 181.8 %reduce-scatter.4.cloned.1.call-done = bf16[448,1024]{1,0:T(8,128)(2,1)} async-done(((bf16[3584,1024]{1,0:T(8,128)(2,1)}), bf16[448,1024]{1,0:T(8,128)(2,1)}) %reduce-scatter.4.cloned.1.call-update) | async-done | bytes 917520
  265.0 36.1 %all-reduce.2.cloned.1.call-done = bf16[448,1024]{0,1:T(8,128)(2,1)} async-done(((bf16[448,1024]{0,1:T(8,128)(2,1)}), bf16[448,1024]{0,1:T(8,128)(2,1)}) %all-reduce.2.cloned.1.call-update) | async-done | bytes 917520 | tf_op jit(solution)/shard_map/psum | solution.py:98
  305.3 22.1 %psum.31 = f32[]{:T(128)} all-reduce(f32[]{:T(128)} %fusion.3), channel_id=1, replica_groups=mesh['rep'=4,'shard'=8] {'shard'}, use_global_device_ids=true, to_apply=%region_5.0 | all-reduce | flops 1 | bytes 8 | tf_op jit(solution)/shard_map/psum | solution.py:99
  328.2 3.0 fusion.36
  331.2 3.6 copy.33
  334.8 2.7 reshape.40
  340.7 5.3 %broadcast_in_dim.14 = bf16[1,448,2048]{2,1,0:T(8,128)(2,1)} reshape(bf16[448,4,2,256]{3,2,1,0:T(2,128)(2,1)} %broadcast_in_dim.6) | data formatting | bytes 3670016 | tf_op jit(solution)/shard_map/broadcast_in_dim | solution.py:52
  346.0 10.7 %copy.35 = bf16[1,448,2048]{1,0,2:T(2,128)(2,1)} copy(bf16[1,448,2048]{2,1,0:T(8,128)(2,1)} %broadcast_in_dim.14) | data formatting | bytes 3670016 | tf_op jit(solution)/shard_map/broadcast_in_dim | solution.py:52
  357.2 15.4 %reduce = bf16[2048,448]{1,0:T(8,128)(2,1)} reduce(bf16[2048,1,448]{2,1,0:T(2,128)(2,1)} %bitcast.84, bf16[]{:T(256)} %broadcast.50), dimensions={1}, to_apply=%bitcast.77.reduce_sub_computation | reduce | bytes 3670018
  372.6 6.8 %reshape.57 = bf16[8,2,57344]{2,1,0:T(2,128)(2,1)} reshape(bf16[2048,448]{1,0:T(8,128)(2,1)} %reduce) | data formatting | bytes 3670016
  379.4 4.3 all-to-all-start
  383.7 11.1 %copy.46 = bf16[2,448,8,256]{3,1,2,0:T(8,128)(2,1)} copy(bf16[2,448,8,256]{1,0,3,2:T(2,128)(2,1)} %bitcast.27) | data formatting | bytes 7340032 | tf_op jit(solution)/shard_map/all_to_all | solution.py:72
  396.6 25.9 %all-to-all-done = bf16[8,2,57344]{2,1,0:T(2,128)(2,1)} async-done(((bf16[8,2,57344]{2,1,0:T(2,128)(2,1)}), bf16[8,2,57344]{2,1,0:T(2,128)(2,1)}, u32[]{:S(2)}, u32[]{:S(2)}) %all-to-all-start) | async-done | bytes 1835040 | tf_op jit(solution)/shard_map/all_to_all | solution.py:102
  422.5 7.2 %reshape.58 = bf16[2048,1,448]{2,1,0:T(2,128)(2,1)} reshape(bf16[8,2,57344]{2,1,0:T(2,128)(2,1)} %all-to-all-done) | data formatting | bytes 3670016
  429.6 2.8 copy.50
  432.4 3.0 copy.43
  438.0 2.9 pad_maximum_fusion
  (37 shorter events, 27.3 us)
Async XLA Ops:
  7.2 36.8 %copy-start = (bf16[448,3584]{1,0:T(8,128)(2,1)S(1)}, bf16[448,3584]{1,0:T(8,128)(2,1)}, u32[]{:S(2)}) copy-start(bf16[448,3584]{1,0:T(8,128)(2,1)} %param.10) | copy-start | bytes 9633796
  7.2 255.6 %reduce-scatter.4.cloned.1.call-start = ((), (), s32[]{:S(2)}) async-start(), calls=%async_computation.4 | async-start | bytes 8257536
  76.4 303.0 %all-to-all-start.1 = ((bf16[2,448,2048]{1,0,2:T(2,128)(2,1)}), bf16[2,448,2048]{1,0,2:T(2,128)(2,1)}, u32[]{:S(2)}, u32[]{:S(2)}) async-start(bf16[2,448,2048]{1,0,2:T(2,128)(2,1)} %bitcast.83), calls=%async_computation.1 | async-start | bytes 8388608 | tf_op jit(solution)/shard_map/all_to_all | solution.py:72
  80.9 220.2 %all-reduce.2.cloned.1.call-start = ((), (), s32[]{:S(2)}) async-start(), calls=%async_computation.3 | async-start | bytes 2097152 | tf_op jit(solution)/shard_map/psum | solution.py:98
  265.0 38.4 %slice-start = ((f32[3,448,1024]{2,1,0:T(8,128)}), f32[1,448,1024]{2,1,0:T(8,128)S(1)}, s32[]{:S(2)}) async-start(f32[3,448,1024]{2,1,0:T(8,128)} %param.19), calls=%async_computation.5 | async-start | bytes 3670016 | tf_op jit(solution)/shard_map/slice | solution.py:101
  303.5 24.7 %copy-start.3 = (bf16[448,1024]{0,1:T(8,128)(2,1)S(1)}, bf16[448,1024]{0,1:T(8,128)(2,1)}, u32[]{:S(2)}) copy-start(bf16[448,1024]{0,1:T(8,128)(2,1)} %all-reduce.2.cloned.1.call-done) | copy-start | bytes 2752516
  379.4 43.1 %all-to-all-start = ((bf16[8,2,57344]{2,1,0:T(2,128)(2,1)}), bf16[8,2,57344]{2,1,0:T(2,128)(2,1)}, u32[]{:S(2)}, u32[]{:S(2)}) async-start(bf16[8,2,57344]{2,1,0:T(2,128)(2,1)} %reshape.57), calls=%async_computation | async-start | bytes 3670016 | tf_op jit(solution)/shard_map/all_to_all | solution.py:102
  435.4 2.6 copy-start.2
  438.0 3.1 copy-start.1
Sparse Core Ops, SparseCore 0:
  62.0 200.6 reduce-scatter.3
  265.7 35.3 all-reduce.1
